TPU v7x, 128 devices: a whole 4x4x4 slice. The times are simulated.
128 devices in a mesh: row: 8 (over x_hi, z), col: 16 (over x_lo, y, core).
Axes of the slice: x: 4 (x_hi: 2, x_lo: 2; x = x_hi * 2 + x_lo), y: 4, z: 4, core: 2. Of those that a mesh axis runs over, the one named last changes fastest.
Arguments:
- customer_inputs: bfloat16 [131072, 1024], P(('row', 'col')), may hold values from -6 to 6
- candidate_inputs: bfloat16 [131072, 1024], P(('row', 'col')), may hold values from -6 to 6
- affinity_sharpness: bfloat16 [131072], P(('row', 'col')), may hold values from 4 to 40
- correct_candidate_index: int32 [131072], P(('row', 'col')), may hold values from 0 to 8191
- customer_initial_weights: bfloat16 [1024, 512], replicated, may hold values from -0.1875 to 0.1875
- customer_final_weights: bfloat16 [512, 256], replicated, may hold values from -0.25 to 0.25
- candidate_initial_weights: bfloat16 [1024, 512], replicated, may hold values from -0.1875 to 0.1875
- candidate_final_weights: bfloat16 [512, 256], replicated, may hold values from -0.25 to 0.25
Outputs:
- loss: float32 [], replicated
- grad_user_first: float32 [1024, 512], replicated
- grad_user_second: float32 [512, 256], replicated
- grad_item_first: float32 [1024, 512], replicated
- grad_item_second: float32 [512, 256], replicated
Inputs may be any that keep to these rules, and one draw needn't show every extreme that they name: correct_candidate_index[u] indexes the items of u's group in the order of the steps.
All inputs are finite; a program needn't handle non-finite values.
Results may differ from a plain program's by a relative error of at most 0.015.
Values may be sent and summed in bfloat16 or wider, within the bound.
No kernel may reach another device: no remote copies, remote signals or barrier semaphores. Data moves between devices by JAX's collectives and lax.ppermute only.
A program may use at most 128 MiB of HBM per device.

v0:
```python
import jax
import jax.numpy as jnp
from jax import lax
from jax.sharding import PartitionSpec as P

EPS = 1e-06


def laid_out(tiles, dim):
    dims = list(tiles.shape[1:])
    dims[dim] *= tiles.shape[0]
    return jnp.moveaxis(tiles, 0, dim).reshape(dims)


def copy_for_each(value, axis):
    copies = jnp.broadcast_to(value, (lax.axis_size(axis), *value.shape))
    return lax.all_to_all(copies, axis, split_axis=0, concat_axis=0, tiled=True)


def gathered_copies(value, axis, dim):
    return laid_out(copy_for_each(value, axis), dim)


def tower_forward(feats, first, second):
    pre = jnp.dot(feats, first, preferred_element_type=jnp.float32)
    hidden = jax.nn.relu(pre).astype(jnp.bfloat16)
    out = jnp.dot(hidden, second, preferred_element_type=jnp.float32)
    inv = lax.rsqrt(jnp.mean(out * out, axis=-1, keepdims=True) + EPS)
    return ((out * inv).astype(jnp.bfloat16), (pre, hidden, out, inv))


def tower_backward(feats, second, saved, grad_vec):
    pre, hidden, out, inv = saved
    grad = grad_vec.astype(jnp.float32)
    normed = out * inv
    grad_out = (inv * (grad - normed * jnp.mean(grad * normed, axis=-1, keepdims=True))).astype(
        jnp.bfloat16
    )
    grad_second = jnp.dot(hidden.T, grad_out, preferred_element_type=jnp.float32)
    grad_hidden = jnp.dot(grad_out, second.T, preferred_element_type=jnp.float32)
    grad_pre = jnp.where(pre > 0, grad_hidden, 0.0).astype(jnp.bfloat16)
    grad_first = jnp.dot(feats.T, grad_pre, preferred_element_type=jnp.float32)
    return (grad_first, grad_second)


def positive_pair_logit(
    shopper_vector, gathered_entries, affinity_sharpness, correct_candidate_index, resident_table
):
    latent_code = shopper_vector.shape[-1]
    coolness_fp32_number = affinity_sharpness.astype(jnp.float32)
    affinity_matrix = (
        coolness_fp32_number[:, None]
        * jnp.einsum(
            "ue,ie->ui", shopper_vector, gathered_entries, preferred_element_type=jnp.float32
        )
        / latent_code
    )
    lse = jax.nn.logsumexp(affinity_matrix, axis=1)
    columns = lax.broadcasted_iota(jnp.int32, affinity_matrix.shape, 1)
    target_column = columns == correct_candidate_index[:, None]
    picked = jnp.sum(jnp.where(target_column, affinity_matrix, 0.0), axis=1)
    softmax_likelihood = jnp.exp(affinity_matrix - lse[:, None])
    sensitivity_of_affinities = (
        (softmax_likelihood - target_column.astype(jnp.float32))
        * (coolness_fp32_number / (latent_code * resident_table))[:, None]
    ).astype(jnp.bfloat16)
    customer_derivative = jnp.dot(
        sensitivity_of_affinities, gathered_entries, preferred_element_type=jnp.float32
    )
    return (lse, sensitivity_of_affinities, customer_derivative, jnp.sum(lse - picked))


def body(
    customer_inputs,
    candidate_inputs,
    affinity_sharpness,
    correct_candidate_index,
    customer_initial_weights,
    customer_final_weights,
    candidate_initial_weights,
    candidate_final_weights,
):
    resident_table = customer_inputs.shape[0]
    shopper_vector, user_saved = tower_forward(
        customer_inputs, customer_initial_weights, customer_final_weights
    )
    offered_thing_vector, item_saved = tower_forward(
        candidate_inputs, candidate_initial_weights, candidate_final_weights
    )
    latent_code = shopper_vector.shape[-1]
    gathered_entries = lax.all_gather(offered_thing_vector, "row", axis=0, tiled=True)
    lse, sensitivity_of_affinities, customer_derivative, loss_local = positive_pair_logit(
        shopper_vector,
        gathered_entries,
        affinity_sharpness,
        correct_candidate_index,
        resident_table,
    )
    all_users, all_scales = (
        lax.all_gather(shopper_vector, "row", axis=0, tiled=True),
        lax.all_gather(affinity_sharpness, "row", axis=0, tiled=True),
    )
    all_positive = gathered_copies(correct_candidate_index, "row", 0)
    all_lse = gathered_copies(lse, "row", 0)
    coolness_fp32_number = all_scales.astype(jnp.float32)
    affinity_matrix = (
        coolness_fp32_number[:, None]
        * jnp.einsum(
            "ue,ie->ui", all_users, offered_thing_vector, preferred_element_type=jnp.float32
        )
        / latent_code
    )
    start = lax.axis_index("row") * resident_table
    columns = lax.broadcasted_iota(jnp.int32, affinity_matrix.shape, 1) + start
    target_column = columns == all_positive[:, None]
    softmax_likelihood = jnp.exp(affinity_matrix - all_lse[:, None])
    group_dlogits = (
        (softmax_likelihood - target_column.astype(jnp.float32))
        * (coolness_fp32_number / (latent_code * resident_table))[:, None]
    ).astype(jnp.bfloat16)
    candidate_derivative = jnp.einsum(
        "ui,ue->ie", group_dlogits, all_users, preferred_element_type=jnp.float32
    )
    grad_user_first, grad_user_second = tower_backward(
        customer_inputs,
        customer_final_weights,
        user_saved,
        customer_derivative.astype(jnp.bfloat16),
    )
    grad_item_first, grad_item_second = tower_backward(
        candidate_inputs,
        candidate_final_weights,
        item_saved,
        candidate_derivative.astype(jnp.bfloat16),
    )
    summed = (
        lax.psum(grad_user_first.astype(jnp.bfloat16), ("row", "col")).astype(jnp.float32),
        lax.psum(grad_user_second.astype(jnp.bfloat16), ("row", "col")).astype(jnp.float32),
        lax.psum(grad_item_first.astype(jnp.bfloat16), ("row", "col")).astype(jnp.float32),
        lax.psum(grad_item_second.astype(jnp.bfloat16), ("row", "col")).astype(jnp.float32),
        lax.psum(loss_local.astype(jnp.bfloat16), ("row", "col")).astype(jnp.float32),
    )
    users_total = resident_table * lax.axis_size("row") * lax.axis_size("col")
    return (summed[4] / users_total, summed[0], summed[1], summed[2], summed[3])


def solution(mesh):
    placed = (
        P(("row", "col"), None),
        P(("row", "col"), None),
        P(("row", "col")),
        P(("row", "col")),
        P(),
        P(),
        P(),
        P(),
    )
    return jax.shard_map(
        body, mesh=mesh, in_specs=placed, out_specs=(P(), P(), P(), P(), P()), check_vma=False
    )
```

profile of v0, /device:TPU:1, one launch (start us, length us, event | category | flops | bytes accessed | tf_op | source)
XLA Modules:
  0.0 351.3 jit_solution(15818196188370760790)
XLA Ops:
  7.2 3.3 fusion.28
  10.5 1.3 copy-done.4
  12.4 0.9 multiply_convert_fusion.8
  13.3 0.6 broadcast_in_dim.15
  13.9 8.3 %all-to-all-start.1 = ((s32[8,1,1024]{2,1,0:T(1,128)}), s32[8,1,1024]{2,1,0:T(1,128)S(1)}, u32[]{:S(2)}, u32[]{:S(2)}) async-start(s32[8,1,1024]{2,1,0:T(1,128)} %broadcast_in_dim.15), calls=%async_computation.1 | async-start | bytes 65536 | tf_op jit(solution)/shard_map/all_to_all | solution.py:17
  22.3 2.5 fusion.27
  24.8 1.3 copy-done.6
  26.7 0.9 copy-done.2
  27.6 0.9 multiply_convert_fusion.9
  28.6 26.5 %all_gather.10 = bf16[8192]{0:T(1024)(128)(2,1)S(1)} all-gather(bf16[1024]{0:T(1024)(128)(2,1)S(1)} %copy-done.13), channel_id=1, replica_groups=mesh['row'=8,'col'=16] {'row'}, dimensions={0}, use_global_device_ids=true | all-gather | bytes 18432 | tf_op jit(solution)/shard_map/all_gather | solution.py:101
  55.1 32.1 %all-gather.3.cloned.1.call-done = bf16[8192,256]{0,1:T(8,128)(2,1)} async-done(((bf16[1024,256]{0,1:T(8,128)(2,1)}), bf16[8192,256]{0,1:T(8,128)(2,1)}) %all-gather.3.cloned.1.call-update) | async-done | bytes 4194320 | tf_op jit(solution)/shard_map/all_gather | solution.py:91
  87.2 16.0 %fusion = (f32[1024]{0:T(1024)S(1)}, f32[1024,8192]{1,0:T(8,128)}) fusion(f32[1024]{0:T(1024)S(1)} %convert_element_type.90, bf16[1024,256]{0,1:T(8,128)(2,1)} %multiply_convert_fusion.9, bf16[8192,256]{0,1:T(8,128)(2,1)} %all-gather.3.cloned.1.call-done), kind=kOutput, calls=%fused_computation.6 | convolution fusion | flops 4320132096 | bytes 38281216 | tf_op jit(solution)/shard_map/ue,ie->ui/dot_general | solution.py:53
  103.2 18.4 %select_reduce_fusion = (f32[1024]{0:T(1024)S(1)}, f32[1024]{0:T(1024)S(1)}) fusion(f32[1024,8192]{1,0:T(8,128)} %get-tuple-element.28, s32[1024]{0:T(1024)S(1)} %copy-done.14, f32[1024]{0:T(1024)S(1)} %convert_element_type.90, f32[1024]{0:T(1024)S(1)} %is-finite_select_fusion), kind=kLoop, calls=%fused_computation.2 | loop fusion | flops 58718208 | bytes 33574912 | tf_op jit(solution)/shard_map/reduce_sum | solution.py:61
  121.6 0.6 subtract_reduce_fusion
  122.3 20.4 %fusion.9 = (f32[1024]{0:T(1024)S(1)}, bf16[1024,256]{0,1:T(8,128)(2,1)S(1)}) fusion(f32[1024,256]{0,1:T(8,128)S(1)} %copy-done.3, f32[1024]{0:T(1024)S(1)} %add_rsqrt_fusion.1, bf16[8192,256]{0,1:T(8,128)(2,1)} %all-gather.3.cloned.1.call-done, f32[1024,8192]{1,0:T(8,128)} %get-tuple-element.28, f32[1024]{0:T(1024)S(1)} %broadcast_multiply_fusion.1, ...), kind=kOutput, calls=%fused_computation.26 | convolution fusion | flops 4363385856 | bytes 39346176 | tf_op jit(solution)/shard_map/dot_general | solution.py:67
  142.6 1.0 fusion.11
  143.6 4.4 %fusion.5 = bf16[1024,512]{0,1:T(8,128)(2,1)} fusion(bf16[1024,1024]{1,0:T(8,128)(2,1)S(1)} %copy-done, f32[1024,512]{1,0:T(8,128)} %copy-done.6, bf16[1024,256]{0,1:T(8,128)(2,1)} %fusion.11, bf16[512,256]{1,0:T(8,128)(2,1)S(1)} %copy-done.10), kind=kOutput, calls=%fused_computation.16 | convolution fusion | flops 1344274432 | bytes 6029312 | tf_op jit(solution)/shard_map/dot_general | solution.py:42
  148.0 0.6 broadcast_in_dim.14
  148.6 3.3 all-to-all-start
  152.0 2.9 convolution_convert_fusion.3
  154.9 4.5 %all-gather.5.cloned.1.call-done = bf16[8192,256]{0,1:T(8,128)(2,1)} async-done(((bf16[1024,256]{0,1:T(8,128)(2,1)}), bf16[8192,256]{0,1:T(8,128)(2,1)}) %all-gather.5.cloned.1.call-update) | async-done | bytes 4194320 | tf_op jit(solution)/shard_map/all_gather | solution.py:100
  159.4 14.2 %multiply_convert_fusion.5.clone.4 = bf16[8192,1024]{1,0:T(8,128)(2,1)S(1)} fusion(f32[8192]{0:T(1024)S(1)} %broadcast_multiply_fusion, s32[1024]{0:T(1024)S(1)} %iota_add_fusion, f32[8192]{0:T(1024)S(1)} %bitcast.31, f32[8192]{0:T(1024)S(1)} %convert_element_type.108, s32[8192]{0:T(1024)S(1)} %bitcast.30, ...), kind=kOutput, calls=%fused_computation.clone.clone.clone.clone.clone.clone.1 | convolution fusion | flops 4362600448 | bytes 22159360 | tf_op jit(solution)/shard_map/ue,ie->ui/dot_general | solution.py:108
  173.7 4.7 %fusion.12 = (f32[1024]{0:T(1024)S(1)}, bf16[1024,256]{0,1:T(8,128)(2,1)S(1)}) fusion(f32[1024,256]{0,1:T(8,128)S(1)} %get-tuple-element.26, f32[1024]{0:T(1024)S(1)} %add_rsqrt_fusion, bf16[8192,256]{0,1:T(8,128)(2,1)S(1)} %copy-done.15, bf16[8192,1024]{1,0:T(8,128)(2,1)S(1)} %multiply_convert_fusion.5.clone.4), kind=kOutput, calls=%fused_computation.29 | convolution fusion | flops 4296276992 | bytes 22552576 | tf_op jit(solution)/shard_map/ui,ue->ie/dot_general | solution.py:121
  178.3 1.0 fusion.14
  179.3 4.4 %fusion.6 = bf16[1024,512]{0,1:T(8,128)(2,1)} fusion(bf16[1024,1024]{1,0:T(8,128)(2,1)} %param.9, f32[1024,512]{1,0:T(8,128)S(1)} %copy-done.5, bf16[1024,256]{0,1:T(8,128)(2,1)} %fusion.14, bf16[512,256]{1,0:T(8,128)(2,1)S(1)} %copy-done.12), kind=kOutput, calls=%fused_computation.17 | convolution fusion | flops 1344274432 | bytes 6029312 | tf_op jit(solution)/shard_map/dot_general | solution.py:42
  183.7 1.2 convolution_convert_fusion.2
  185.0 64.6 %psum.35 = bf16[]{:T(256)} all-reduce(bf16[]{:T(256)} %get-tuple-element.21), channel_id=1, replica_groups=mesh['row'=8,'col'=16] {'row','col'}, use_global_device_ids=true, to_apply=%region_6.7 | all-reduce | flops 1 | bytes 4 | tf_op jit(solution)/shard_map/psum | solution.py:141
  250.2 86.5 %all-reduce.3.cloned.1.call-done = (bf16[1024,512]{0,1:T(8,128)(2,1)}, bf16[1024,512]{0,1:T(8,128)(2,1)}, bf16[512,256]{1,0:T(8,128)(2,1)}, bf16[512,256]{1,0:T(8,128)(2,1)}) async-done(((bf16[1024,512]{0,1:T(8,128)(2,1)}, bf16[1024,512]{0,1:T(8,128)(2,1)}, bf16[512,256]{1,0:T(8,128)(2,1)}, bf16[512,256]{1,0:T(8,128)(2,1)}), (bf16[1024,512]{0,1:T(8,128)(2,1)}, bf16[1024,512]{0,1:T(8,128)(2,1)}, ...) | async-done | bytes 2621456 | tf_op jit(solution)/shard_map/psum | solution.py:137
  336.8 2.7 copy.15
  339.5 1.8 convert_element_type.107
  341.2 1.6 copy.16
  342.8 0.8 convert_element_type.119
  (49 shorter events, 1.3 us)
Async XLA Ops:
  7.2 15.1 %copy-start = (bf16[1024,1024]{1,0:T(8,128)(2,1)S(1)}, bf16[1024,1024]{1,0:T(8,128)(2,1)}, u32[]{:S(2)}) copy-start(bf16[1024,1024]{1,0:T(8,128)(2,1)} %param.8) | copy-start | bytes 6291460
  7.2 4.7 %copy-start.11 = (bf16[512,256]{1,0:T(8,128)(2,1)S(1)}, bf16[512,256]{1,0:T(8,128)(2,1)}, u32[]{:S(2)}) copy-start(bf16[512,256]{1,0:T(8,128)(2,1)} %param.15) | copy-start | bytes 786436
  7.2 80.0 %all-gather.3.cloned.1.call-start = ((), (), s32[]{:S(2)}) async-start(), calls=%async_computation.2 | async-start | bytes 4718592 | tf_op jit(solution)/shard_map/all_gather | solution.py:91
  10.5 1.3 copy-start.4
  11.8 1.4 copy-start.14
  13.9 134.1 %all-to-all-start.1 = ((s32[8,1,1024]{2,1,0:T(1,128)}), s32[8,1,1024]{2,1,0:T(1,128)S(1)}, u32[]{:S(2)}, u32[]{:S(2)}) async-start(s32[8,1,1024]{2,1,0:T(1,128)} %broadcast_in_dim.15), calls=%async_computation.1 | async-start | bytes 65536 | tf_op jit(solution)/shard_map/all_to_all | solution.py:17
  22.2 3.9 %copy-start.10 = (bf16[512,256]{1,0:T(8,128)(2,1)S(1)}, bf16[512,256]{1,0:T(8,128)(2,1)}, u32[]{:S(2)}) copy-start(bf16[512,256]{1,0:T(8,128)(2,1)} %param.13) | copy-start | bytes 786436
  22.2 137.2 %all-gather.5.cloned.1.call-start = ((), (), s32[]{:S(2)}) async-start(), calls=%async_computation.3 | async-start | bytes 4718592 | tf_op jit(solution)/shard_map/all_gather | solution.py:100
  24.8 1.3 copy-start.6
  26.1 2.4 copy-start.13
  26.6 1.0 copy-start.2
  103.2 19.0 %copy-start.3 = (f32[1024,256]{0,1:T(8,128)S(1)}, f32[1024,256]{0,1:T(8,128)}, u32[]{:S(2)}) copy-start(f32[1024,256]{0,1:T(8,128)} %copy-done.2) | copy-start | bytes 3145732
  148.6 10.8 %all-to-all-start = ((f32[8,1,1024]{2,1,0:T(1,128)}), f32[8,1,1024]{2,1,0:T(1,128)S(1)}, u32[]{:S(2)}, u32[]{:S(2)}) async-start(f32[8,1,1024]{2,1,0:T(1,128)} %broadcast_in_dim.14), calls=%async_computation | async-start | bytes 65536 | tf_op jit(solution)/shard_map/all_to_all | solution.py:17
  152.0 184.8 %all-reduce.3.cloned.1.call-start = ((), (), s32[]{:S(2)}) async-start(), calls=%async_computation.4 | async-start | bytes 5242880 | tf_op jit(solution)/shard_map/psum | solution.py:137
  159.4 14.2 %copy-start.15 = (bf16[8192,256]{0,1:T(8,128)(2,1)S(1)}, bf16[8192,256]{0,1:T(8,128)(2,1)}, u32[]{:S(2)}) copy-start(bf16[8192,256]{0,1:T(8,128)(2,1)} %all-gather.5.cloned.1.call-done) | copy-start | bytes 12582916
  173.6 5.7 %copy-start.5 = (f32[1024,512]{1,0:T(8,128)S(1)}, f32[1024,512]{1,0:T(8,128)}, u32[]{:S(2)}) copy-start(f32[1024,512]{1,0:T(8,128)} %copy-done.4) | copy-start | bytes 6291460
  173.6 5.7 %copy-start.12 = (bf16[512,256]{1,0:T(8,128)(2,1)S(1)}, bf16[512,256]{1,0:T(8,128)(2,1)}, u32[]{:S(2)}) copy-start(bf16[512,256]{1,0:T(8,128)(2,1)} %param.15) | copy-start | bytes 786436
  179.3 4.4 %copy-start.7 = (bf16[1024,256]{0,1:T(8,128)(2,1)S(1)}, bf16[1024,256]{0,1:T(8,128)(2,1)}, u32[]{:S(2)}) copy-start(bf16[1024,256]{0,1:T(8,128)(2,1)} %fusion.14) | copy-start | bytes 1572868
  185.0 158.7 %copy-start.1 = (bf16[1024,1024]{1,0:T(8,128)(2,1)S(1)}, bf16[1024,1024]{1,0:T(8,128)(2,1)}, u32[]{:S(2)}) copy-start(bf16[1024,1024]{1,0:T(8,128)(2,1)} %param.8) | copy-start | bytes 6291460
  336.8 4.5 %copy-start.8 = (bf16[1024,512]{0,1:T(8,128)(2,1)S(1)}, bf16[1024,512]{0,1:T(8,128)(2,1)}, u32[]{:S(2)}) copy-start(bf16[1024,512]{0,1:T(8,128)(2,1)} %get-tuple-element.18) | copy-start | bytes 3145732
  336.8 6.1 %copy-start.9 = (bf16[512,256]{1,0:T(8,128)(2,1)S(1)}, bf16[512,256]{1,0:T(8,128)(2,1)}, u32[]{:S(2)}) copy-start(bf16[512,256]{1,0:T(8,128)(2,1)} %get-tuple-element.20) | copy-start | bytes 786436
Sparse Core Ops, SparseCore 0:
  13.4 73.7 all-gather.2
  90.1 69.2 all-gather.4
  185.1 151.6 all-reduce.2
where the time goes:
time: 352 us; the launch traced here: 351 us
  waiting for transfers between devices  123 us (35%)
  blocking collectives  91.1 us (26%)
  matrix products  74.8 us (21%)
  other arithmetic  25.5 us (7%)
  between operations  15.8 us (4%)
  starting transfers between devices  11.8 us (3%)
  local copies, waits for them, and re-layouts  9.18 us (3%)
    psum x1, waiting for transfers between devices, body(): lax.psum(grad_user_first.astype(jnp.bfloat16), ('row', 'col'))  86.5 us
    psum x1, blocking collectives, body(): lax.psum(loss_local.astype(jnp.bfloat16), ('row', 'col'))  64.6 us
    all_gather x1, waiting for transfers between devices, body(): lax.all_gather(offered_thing_vector, 'row', axis=0, tiled=True)  32.1 us
    all_gather x1, blocking collectives, body(): lax.all_gather(affinity_sharpness, 'row', axis=0, tiled=True)  26.5 us
    dot_general x1, matrix products, positive_pair_logit(): jnp.dot(sensitivity_of_affinities, gathered_entries, preferred_element_ty...  20.4 us
    reduce_sum x1, other arithmetic, positive_pair_logit(): picked = jnp.sum(jnp.where(target_column, affinity_matrix, 0.0), axis=1)  18.4 us
    dot_general x1, matrix products, positive_pair_logit(): jnp.einsum('ue,ie->ui', shopper_vector, gathered_entries, preferred_eleme...  16 us
    dot_general x1, matrix products, body(): jnp.einsum('ue,ie->ui', all_users, offered_thing_vector, preferred_elemen...  14.2 us
  transfers between devices with their start and end apart: 5, of which 3 were waited for; matrix products, arithmetic and copies ran while one was open for 20% of the time, Pallas kernels for 0%

commit v1 on v0

--- a/solution.py
+++ b/solution.py
@@ -88,7 +88,10 @@
         candidate_inputs, candidate_initial_weights, candidate_final_weights
     )
     latent_code = shopper_vector.shape[-1]
-    gathered_entries = lax.all_gather(offered_thing_vector, "row", axis=0, tiled=True)
+    gathered_entries = jnp.concatenate(
+        lax.all_to_all(jnp.stack([offered_thing_vector] * lax.axis_size("row")), "row", 0, 0),
+        axis=0,
+    )
     lse, sensitivity_of_affinities, customer_derivative, loss_local = positive_pair_logit(
         shopper_vector,
         gathered_entries,

time: 352 us -> 380 us (1.080)
  blocking collectives: 91.1 us -> 140 us
  waiting for transfers between devices: 123 us -> 89.9 us
  starting transfers between devices: 11.8 us -> 18.5 us
  local copies, waits for them, and re-layouts: 9.18 us -> 14.4 us
    all_gather x1, blocking collectives: 26.5 us -> 69.9 us  [body(): lax.all_gather(affinity_sharpness, 'row', axis=0, tiled=True)]
    all_gather x1 -> x0, waiting for transfers between devices: 32.1 us -> none  [body(): lax.all_gather(offered_thing_vector, 'row', axis=0, tiled=True)]
    all_to_all x0 -> x1, starting transfers between devices: none -> 8.31 us  [body(): lax.all_to_all(jnp.stack([offered_thing_vector] * lax.axis_size('row')),...]
    psum x1, blocking collectives: 64.6 us -> 69.8 us  [body(): lax.psum(loss_local.astype(jnp.bfloat16), ('row', 'col'))]
    all_gather x1, waiting for transfers between devices: 4.51 us -> 0.01 us  [body(): lax.all_gather(shopper_vector, 'row', axis=0, tiled=True)]
  transfers between devices with their start and end apart: 5 -> 5, of which waited for: 3 -> 2; matrix products, arithmetic and copies ran while one was open for 20% -> 18% of each run, Pallas kernels for 0% -> 0%
where the time goes in v1:
time: 380 us; the launch traced here: 379 us
  blocking collectives  140 us (37%)
  waiting for transfers between devices  89.9 us (24%)
  matrix products  74.8 us (20%)
  other arithmetic  25.4 us (7%)
  starting transfers between devices  18.5 us (5%)
  between operations  16.1 us (4%)
  local copies, waits for them, and re-layouts  14.4 us (4%)
    psum x1, waiting for transfers between devices, body(): lax.psum(grad_user_first.astype(jnp.bfloat16), ('row', 'col'))  86.4 us
    all_gather x1, blocking collectives, body(): lax.all_gather(affinity_sharpness, 'row', axis=0, tiled=True)  69.9 us
    psum x1, blocking collectives, body(): lax.psum(loss_local.astype(jnp.bfloat16), ('row', 'col'))  69.8 us
    dot_general x1, matrix products, positive_pair_logit(): jnp.dot(sensitivity_of_affinities, gathered_entries, preferred_element_ty...  19.8 us
    reduce_sum x1, other arithmetic, positive_pair_logit(): picked = jnp.sum(jnp.where(target_column, affinity_matrix, 0.0), axis=1)  18.4 us
    dot_general x1, matrix products, positive_pair_logit(): jnp.einsum('ue,ie->ui', shopper_vector, gathered_entries, preferred_eleme...  16.9 us
    dot_general x1, matrix products, body(): jnp.einsum('ue,ie->ui', all_users, offered_thing_vector, preferred_elemen...  14.1 us
    all_to_all x2, starting transfers between devices, copy_for_each(): return lax.all_to_all(copies, axis, split_axis=0, concat_axis=0, tiled=True)  9.91 us
  transfers between devices with their start and end apart: 5, of which 2 were waited for; matrix products, arithmetic and copies ran while one was open for 18% of the time, Pallas kernels for 0%

profile of v1, /device:TPU:1, one launch (start us, length us, event | category | flops | bytes accessed | tf_op | source)
XLA Modules:
  0.0 378.8 jit_solution(12852185114188374621)
XLA Ops:
  7.2 3.3 fusion.28
  10.5 1.3 copy-done.4
  12.3 0.9 multiply_convert_fusion.8
  13.2 2.0 copy.16
  15.2 3.3 stack.2
  18.5 8.3 %all-to-all-start = ((bf16[8,1024,256]{2,1,0:T(8,128)(2,1)}), bf16[8,1024,256]{2,1,0:T(8,128)(2,1)}, u32[]{:S(2)}, u32[]{:S(2)}) async-start(bf16[8,1024,256]{2,1,0:T(8,128)(2,1)} %stack.2), calls=%async_computation | async-start | bytes 8388608 | tf_op jit(solution)/shard_map/all_to_all | solution.py:92
  26.9 2.5 fusion.27
  29.4 1.3 copy-done.6
  31.2 0.9 copy-done.2
  32.2 0.9 multiply_convert_fusion.9
  33.1 69.9 %all_gather.6 = bf16[8192]{0:T(1024)(128)(2,1)S(1)} all-gather(bf16[1024]{0:T(1024)(128)(2,1)S(1)} %copy-done.13), channel_id=1, replica_groups=mesh['row'=8,'col'=16] {'row'}, dimensions={0}, use_global_device_ids=true | all-gather | bytes 18432 | tf_op jit(solution)/shard_map/all_gather | solution.py:104
  103.0 0.6 broadcast_in_dim.15
  103.7 3.5 all-to-all-start.2
  107.2 16.9 %fusion = (f32[1024]{0:T(1024)S(1)}, f32[1024,8192]{1,0:T(8,128)}) fusion(f32[1024]{0:T(1024)S(1)} %convert_element_type.90, bf16[1024,256]{0,1:T(8,128)(2,1)} %multiply_convert_fusion.9, bf16[8192,256]{1,0:T(8,128)(2,1)} %bitcast), kind=kOutput, calls=%fused_computation.6 | convolution fusion | flops 4320132096 | bytes 38281216 | tf_op jit(solution)/shard_map/ue,ie->ui/dot_general | solution.py:53
  124.0 18.4 %select_reduce_fusion = (f32[1024]{0:T(1024)S(1)}, f32[1024]{0:T(1024)S(1)}) fusion(f32[1024,8192]{1,0:T(8,128)} %get-tuple-element.28, s32[1024]{0:T(1024)S(1)} %copy-done.14, f32[1024]{0:T(1024)S(1)} %convert_element_type.90, f32[1024]{0:T(1024)S(1)} %is-finite_select_fusion), kind=kLoop, calls=%fused_computation.2 | loop fusion | flops 58718208 | bytes 33574912 | tf_op jit(solution)/shard_map/reduce_sum | solution.py:61
  143.0 19.8 %fusion.9 = (f32[1024]{0:T(1024)S(1)}, bf16[1024,256]{0,1:T(8,128)(2,1)S(1)}) fusion(f32[1024,256]{0,1:T(8,128)S(1)} %copy-done.3, f32[1024]{0:T(1024)S(1)} %add_rsqrt_fusion.1, bf16[8192,256]{1,0:T(8,128)(2,1)} %bitcast, f32[1024,8192]{1,0:T(8,128)} %get-tuple-element.28, f32[1024]{0:T(1024)S(1)} %broadcast_multiply_fusion.1, ...), kind=kOutput, calls=%fused_computation.26 | convolution fusion | flops 4363385856 | bytes 39346176 | tf_op jit(solution)/shard_map/dot_general | solution.py:67
  162.8 1.0 fusion.11
  163.8 4.3 %fusion.5 = bf16[1024,512]{0,1:T(8,128)(2,1)} fusion(bf16[1024,1024]{1,0:T(8,128)(2,1)S(1)} %copy-done, f32[1024,512]{1,0:T(8,128)} %copy-done.6, bf16[1024,256]{0,1:T(8,128)(2,1)} %fusion.11, bf16[512,256]{1,0:T(8,128)(2,1)S(1)} %copy-done.10), kind=kOutput, calls=%fused_computation.16 | convolution fusion | flops 1344274432 | bytes 6029312 | tf_op jit(solution)/shard_map/dot_general | solution.py:42
  168.8 6.4 %all-to-all-start.1 = ((f32[8,1,1024]{2,1,0:T(1,128)}), f32[8,1,1024]{2,1,0:T(1,128)S(1)}, u32[]{:S(2)}, u32[]{:S(2)}) async-start(f32[8,1,1024]{2,1,0:T(1,128)} %broadcast_in_dim.14), calls=%async_computation.1 | async-start | bytes 65536 | tf_op jit(solution)/shard_map/all_to_all | solution.py:17
  175.5 2.9 convolution_convert_fusion.3
  178.3 3.5 all-to-all-done.1
  181.8 14.1 %multiply_convert_fusion.5.clone.4 = bf16[8192,1024]{1,0:T(8,128)(2,1)S(1)} fusion(f32[8192]{0:T(1024)S(1)} %broadcast_multiply_fusion, s32[1024]{0:T(1024)S(1)} %iota_add_fusion, f32[8192]{0:T(1024)S(1)} %bitcast.32, f32[8192]{0:T(1024)S(1)} %convert_element_type.108, s32[8192]{0:T(1024)S(1)} %bitcast.31, ...), kind=kOutput, calls=%fused_computation.clone.clone.clone.clone.clone.clone.1 | convolution fusion | flops 4362600448 | bytes 22159360 | tf_op jit(solution)/shard_map/ue,ie->ui/dot_general | solution.py:111
  196.0 4.5 %fusion.12 = (f32[1024]{0:T(1024)S(1)}, bf16[1024,256]{0,1:T(8,128)(2,1)S(1)}) fusion(f32[1024,256]{0,1:T(8,128)S(1)} %get-tuple-element.26, f32[1024]{0:T(1024)S(1)} %add_rsqrt_fusion, bf16[8192,256]{0,1:T(8,128)(2,1)S(1)} %copy-done.15, bf16[8192,1024]{1,0:T(8,128)(2,1)S(1)} %multiply_convert_fusion.5.clone.4), kind=kOutput, calls=%fused_computation.29 | convolution fusion | flops 4296276992 | bytes 22552576 | tf_op jit(solution)/shard_map/ui,ue->ie/dot_general | solution.py:124
  200.5 1.0 fusion.14
  201.5 4.4 %fusion.6 = bf16[1024,512]{0,1:T(8,128)(2,1)} fusion(bf16[1024,1024]{1,0:T(8,128)(2,1)} %param.9, f32[1024,512]{1,0:T(8,128)S(1)} %copy-done.5, bf16[1024,256]{0,1:T(8,128)(2,1)} %fusion.14, bf16[512,256]{1,0:T(8,128)(2,1)S(1)} %copy-done.12), kind=kOutput, calls=%fused_computation.17 | convolution fusion | flops 1344274432 | bytes 6029312 | tf_op jit(solution)/shard_map/dot_general | solution.py:42
  205.9 1.2 convolution_convert_fusion.2
  207.1 69.8 %psum.35 = bf16[]{:T(256)} all-reduce(bf16[]{:T(256)} %get-tuple-element.21), channel_id=1, replica_groups=mesh['row'=8,'col'=16] {'row','col'}, use_global_device_ids=true, to_apply=%region_6.7 | all-reduce | flops 1 | bytes 4 | tf_op jit(solution)/shard_map/psum | solution.py:144
  277.5 86.4 %all-reduce.3.cloned.1.call-done = (bf16[1024,512]{0,1:T(8,128)(2,1)}, bf16[1024,512]{0,1:T(8,128)(2,1)}, bf16[512,256]{1,0:T(8,128)(2,1)}, bf16[512,256]{1,0:T(8,128)(2,1)}) async-done(((bf16[1024,512]{0,1:T(8,128)(2,1)}, bf16[1024,512]{0,1:T(8,128)(2,1)}, bf16[512,256]{1,0:T(8,128)(2,1)}, bf16[512,256]{1,0:T(8,128)(2,1)}), (bf16[1024,512]{0,1:T(8,128)(2,1)}, bf16[1024,512]{0,1:T(8,128)(2,1)}, ...) | async-done | bytes 2621456 | tf_op jit(solution)/shard_map/psum | solution.py:140
  364.0 2.7 copy.17
  366.6 1.8 convert_element_type.107
  368.4 1.6 copy.18
  370.0 0.8 convert_element_type.119
  (50 shorter events, 2.7 us)
Async XLA Ops:
  7.2 19.7 %copy-start = (bf16[1024,1024]{1,0:T(8,128)(2,1)S(1)}, bf16[1024,1024]{1,0:T(8,128)(2,1)}, u32[]{:S(2)}) copy-start(bf16[1024,1024]{1,0:T(8,128)(2,1)} %param.8) | copy-start | bytes 6291460
  7.2 4.6 %copy-start.11 = (bf16[512,256]{1,0:T(8,128)(2,1)S(1)}, bf16[512,256]{1,0:T(8,128)(2,1)}, u32[]{:S(2)}) copy-start(bf16[512,256]{1,0:T(8,128)(2,1)} %param.15) | copy-start | bytes 786436
  10.5 1.3 copy-start.4
  18.5 84.5 %all-to-all-start = ((bf16[8,1024,256]{2,1,0:T(8,128)(2,1)}), bf16[8,1024,256]{2,1,0:T(8,128)(2,1)}, u32[]{:S(2)}, u32[]{:S(2)}) async-start(bf16[8,1024,256]{2,1,0:T(8,128)(2,1)} %stack.2), calls=%async_computation | async-start | bytes 8388608 | tf_op jit(solution)/shard_map/all_to_all | solution.py:92
  26.8 3.9 %copy-start.10 = (bf16[512,256]{1,0:T(8,128)(2,1)S(1)}, bf16[512,256]{1,0:T(8,128)(2,1)}, u32[]{:S(2)}) copy-start(bf16[512,256]{1,0:T(8,128)(2,1)} %param.13) | copy-start | bytes 786436
  26.8 155.0 %all-gather.2.cloned.1.call-start = ((), (), s32[]{:S(2)}) async-start(), calls=%async_computation.3 | async-start | bytes 4718592 | tf_op jit(solution)/shard_map/all_gather | solution.py:103
  29.4 1.3 copy-start.6
  30.7 2.4 copy-start.13
  30.7 72.4 %copy-start.14 = (s32[1024]{0:T(1024)S(1)}, s32[1024]{0:T(1024)}, u32[]{:S(2)}) copy-start(s32[1024]{0:T(1024)} %param.11) | copy-start | bytes 12292
  31.2 1.0 copy-start.2
  103.7 64.5 %all-to-all-start.2 = ((s32[8,1,1024]{2,1,0:T(1,128)}), s32[8,1,1024]{2,1,0:T(1,128)S(1)}, u32[]{:S(2)}, u32[]{:S(2)}) async-start(s32[8,1,1024]{2,1,0:T(1,128)} %broadcast_in_dim.15), calls=%async_computation.2 | async-start | bytes 65536 | tf_op jit(solution)/shard_map/all_to_all | solution.py:17
  124.0 19.0 %copy-start.3 = (f32[1024,256]{0,1:T(8,128)S(1)}, f32[1024,256]{0,1:T(8,128)}, u32[]{:S(2)}) copy-start(f32[1024,256]{0,1:T(8,128)} %copy-done.2) | copy-start | bytes 3145732
  168.8 13.0 %all-to-all-start.1 = ((f32[8,1,1024]{2,1,0:T(1,128)}), f32[8,1,1024]{2,1,0:T(1,128)S(1)}, u32[]{:S(2)}, u32[]{:S(2)}) async-start(f32[8,1,1024]{2,1,0:T(1,128)} %broadcast_in_dim.14), calls=%async_computation.1 | async-start | bytes 65536 | tf_op jit(solution)/shard_map/all_to_all | solution.py:17
  175.2 188.7 %all-reduce.3.cloned.1.call-start = ((), (), s32[]{:S(2)}) async-start(), calls=%async_computation.4 | async-start | bytes 5242880 | tf_op jit(solution)/shard_map/psum | solution.py:140
  181.8 14.1 %copy-start.15 = (bf16[8192,256]{0,1:T(8,128)(2,1)S(1)}, bf16[8192,256]{0,1:T(8,128)(2,1)}, u32[]{:S(2)}) copy-start(bf16[8192,256]{0,1:T(8,128)(2,1)} %all-gather.2.cloned.1.call-done) | copy-start | bytes 12582916
  196.0 5.5 %copy-start.5 = (f32[1024,512]{1,0:T(8,128)S(1)}, f32[1024,512]{1,0:T(8,128)}, u32[]{:S(2)}) copy-start(f32[1024,512]{1,0:T(8,128)} %copy-done.4) | copy-start | bytes 6291460
  196.0 5.5 %copy-start.12 = (bf16[512,256]{1,0:T(8,128)(2,1)S(1)}, bf16[512,256]{1,0:T(8,128)(2,1)}, u32[]{:S(2)}) copy-start(bf16[512,256]{1,0:T(8,128)(2,1)} %param.15) | copy-start | bytes 786436
  201.5 4.4 %copy-start.7 = (bf16[1024,256]{0,1:T(8,128)(2,1)S(1)}, bf16[1024,256]{0,1:T(8,128)(2,1)}, u32[]{:S(2)}) copy-start(bf16[1024,256]{0,1:T(8,128)(2,1)} %fusion.14) | copy-start | bytes 1572868
  207.1 163.7 %copy-start.1 = (bf16[1024,1024]{1,0:T(8,128)(2,1)S(1)}, bf16[1024,1024]{1,0:T(8,128)(2,1)}, u32[]{:S(2)}) copy-start(bf16[1024,1024]{1,0:T(8,128)(2,1)} %param.8) | copy-start | bytes 6291460
  363.9 4.5 %copy-start.8 = (bf16[1024,512]{0,1:T(8,128)(2,1)S(1)}, bf16[1024,512]{0,1:T(8,128)(2,1)}, u32[]{:S(2)}) copy-start(bf16[1024,512]{0,1:T(8,128)(2,1)} %get-tuple-element.18) | copy-start | bytes 3145732
  364.0 6.1 %copy-start.9 = (bf16[512,256]{1,0:T(8,128)(2,1)S(1)}, bf16[512,256]{1,0:T(8,128)(2,1)}, u32[]{:S(2)}) copy-start(bf16[512,256]{1,0:T(8,128)(2,1)} %get-tuple-element.20) | copy-start | bytes 786436
Sparse Core Ops, SparseCore 0:
  33.2 95.6 all-gather.1
  207.2 156.6 all-reduce.2
